TPU v7x, 128 devices: a whole 4x4x4 slice. The times are simulated.
128 devices in a mesh: row: 16 (over z_lo, x, core), col: 8 (over z_hi, y).
Axes of the slice: x: 4, y: 4, z: 4 (z_hi: 2, z_lo: 2; z = z_hi * 2 + z_lo), core: 2. Of those that a mesh axis runs over, the one named last changes fastest.
Arguments:
- density: bfloat16 [64, 5, 256, 256], P('row', None, 'col'), may hold values from -1 to 2, as said below
- pattern: int32 [64, 5], P('row'), may hold values from 0 to 1, as said below
- windows: int32 [256], P(('row', 'col')), may hold values from 0 to 125, as said below
- basis_values: bfloat16 [256, 4096, 384], P(('row', 'col')), may hold values from -6 to 6
- basis_grads: bfloat16 [3, 256, 4096, 384], P(None, ('row', 'col')), may hold values from -48 to 48
- weights: float32 [256, 4096], P(('row', 'col')), may hold values from 0.25 to 4
Outputs:
- purified: bfloat16 [64, 5, 256, 256], P('row', None, 'col')
- xc_matrix: float32 [64, 5, 256, 256], P('row', None, 'col')
- grid_density: float32 [256, 4096], P(('row', 'col'))
Inputs may be any that keep to these rules, and one draw needn't show every extreme that they name: density[i, d] is block (i, i + d - 2) of a symmetric matrix: density[i, d] equals density[i + d - 2, 4 - d] transposed; blocks whose column block lies outside the matrix are 0. pattern[i, d] = pattern[i + d - 2, 4 - d]; it is 1 for d = 1, 2, 3 where block i + d - 2 exists and 0 where it does not. Tile t lies on device t // 2 of the joined axes row+col; if that device has row index q, windows[t] lies between 2 * 4 q - 2 and 2 * 4 q + 2 * 4 - 1.
All inputs are finite; a program needn't handle non-finite values.
Results may differ from a plain program's by a relative error of at most 0.011.
Values may be sent and summed in bfloat16 or wider, within the bound.
A program may use at most 128 MiB of HBM per device.

v0:
```python
import jax
import jax.numpy as jnp
from jax import lax
from jax.sharding import Mesh
from jax.sharding import PartitionSpec as P

ITERS = 2
COL = ("col_0", "col_1")
ROW_COL = ("row", "col_0", "col_1")
slater_cx = 0.7386
kappa_pbe = 0.804
mu_pbe = 0.2195


def shifted_2(value, axis, by):
    length = lax.axis_size(axis)
    pairs = [(i, i + by) for i in range(length) if 0 <= i + by < length]
    return lax.ppermute(value, axis, pairs)


def padded(cells, sides, width):
    for axis, dim in sides:
        count = lax.axis_size(axis)
        ends = count - 1
        head = lax.slice_in_dim(cells, 0, width, axis=dim)
        tail = lax.slice_in_dim(cells, cells.shape[dim] - width, cells.shape[dim], axis=dim)
        cells = jnp.concatenate(
            [
                lax.ppermute(tail, axis, [(i, (i + 1) % count) for i in range(ends)]),
                cells,
                lax.ppermute(head, axis, [((i + 1) % count, i) for i in range(ends)]),
            ],
            axis=dim,
        )
    return cells


def in_order(pieces, dim):
    pieces = jnp.moveaxis(pieces, 0, dim)
    lengths = pieces.shape
    return pieces.reshape(*lengths[:dim], lengths[dim] * lengths[dim + 1], *lengths[dim + 2 :])


def sent_to_all(value, axis):
    length = lax.axis_size(axis)
    return lax.all_to_all(
        jnp.broadcast_to(value[None], (length, *value.shape)), axis, 0, 0, tiled=True
    )


def gather_directly(value, axis, dim):
    return in_order(sent_to_all(value, axis), dim)


def sum_in_order(pieces, axes, sequence):
    inside = pieces.shape[1:]
    pieces = pieces.reshape(*(lax.axis_size(a) for a in axes), *inside)
    pieces = jnp.moveaxis(pieces, sequence, range(len(axes))).reshape(-1, *inside)
    for k in sequence:
        pieces = lax.psum_scatter(pieces, axes[k], scatter_dimension=0, tiled=True)
    return pieces[0]


def cut_along(value, dim, length):
    before, after = (value.shape[:dim], value.shape[dim + 1 :])
    return jnp.moveaxis(value.reshape(*before, length, -1, *after), dim, 0)


def scatter_axes(value, axes, sequence, dim):
    length = lax.axis_size(axes)
    return sum_in_order(cut_along(value, dim, length), axes, sequence)


def energy_sum(point_density, grad_square):
    spread = jnp.sqrt(point_density * point_density + 1.0)
    reduced = grad_square / spread ** (8.0 / 3.0)
    enhance = 1.0 + kappa_pbe - kappa_pbe / (1.0 + mu_pbe * reduced / kappa_pbe)
    return jnp.sum(-slater_cx * spread ** (4.0 / 3.0) * enhance)


def tile_terms(values, grads, quadrature, window_block):
    functions = values.shape[1]
    points = values.shape[0]
    projected = jnp.dot(values, window_block, preferred_element_type=jnp.float32)
    point_density = jnp.sum(projected * values.astype(jnp.float32), axis=1) / functions
    slopes = 2.0 * jnp.sum(projected[None] * grads.astype(jnp.float32), axis=2) / functions
    grad_square = jnp.sum(slopes * slopes, axis=0)
    by_density, by_gradient = jax.grad(energy_sum, argnums=(0, 1))(point_density, grad_square)
    scaled = quadrature / points
    weighted = (0.5 * by_density * scaled)[:, None] * values.astype(jnp.float32)
    weighted = weighted + jnp.sum(
        ((2.0 * by_gradient * scaled)[None] * slopes)[:, :, None] * grads.astype(jnp.float32),
        axis=0,
    )
    weighted = weighted.astype(jnp.bfloat16)
    one_side = lax.dot_general(
        values, weighted, (((0,), (0,)), ((), ())), preferred_element_type=jnp.float32
    )
    return (point_density, one_side + one_side.T)


def band_product(left, right_padded):
    blocks = left.shape[0]
    total = None
    for offset_step in range(5):
        shifted = right_padded[offset_step : offset_step + blocks]
        widened = jnp.pad(shifted, ((0, 0), (2, 2), (0, 0), (0, 0)))
        picked = widened[:, 4 - offset_step : 9 - offset_step]
        term = jnp.einsum(
            "brk,bdkc->bdrc", left[:, offset_step], picked, preferred_element_type=jnp.float32
        )
        total = term if total is None else total + term
    return total


def window_of(band_three, lead, offset, functions):
    paired = lax.dynamic_slice_in_dim(band_three, lead, 2, 0)
    upper = jnp.concatenate([paired[0, 1], paired[0, 2]], axis=1)
    lower = jnp.concatenate([paired[1, 0], paired[1, 1]], axis=1)
    dense = jnp.concatenate([upper, lower], axis=0)
    return lax.dynamic_slice(dense, (offset, offset), (functions, functions))


def spread_term(summed, term, lead, offset):
    width = summed.shape[2]
    dense = lax.dynamic_update_slice(
        jnp.zeros((2 * width, 2 * width), summed.dtype), term, (offset, offset)
    )
    nothing = jnp.zeros((width, width), summed.dtype)
    upper = jnp.stack([nothing, dense[:width, :width], dense[:width, width:]])
    lower = jnp.stack([dense[width:, :width], dense[width:, width:], nothing])
    increment = jnp.stack([upper, lower])
    paired = lax.dynamic_slice_in_dim(summed, lead, 2, 0)
    return lax.dynamic_update_slice_in_dim(summed, paired + increment, lead, 0)


def edge_rows(summed):
    blocks = summed.shape[0] - 2
    from_above = shifted_2(summed[0].astype(jnp.bfloat16), "row", -1).astype(jnp.float32)
    from_below = shifted_2(summed[blocks + 1].astype(jnp.bfloat16), "row", 1).astype(jnp.float32)
    own_rows = summed[1 : blocks + 1]
    return jnp.concatenate(
        [
            own_rows[:1] + from_below[None],
            own_rows[1 : blocks - 1],
            own_rows[blocks - 1 :] + from_above[None],
        ],
        axis=0,
    )


def on_device(density, pattern, windows, basis_values, basis_grads, weights):
    row_index = lax.axis_index("row")
    band_rows = density.shape[0]
    functions = basis_values.shape[2]
    step_size = functions // 3
    kept = (pattern > 0)[:, :, None, None]
    current = jnp.where(kept, density, jnp.zeros_like(density))
    for iteration in range(ITERS):
        near_right = padded(current, (("row", 0),), 2)
        right_full = lax.all_gather(near_right, COL, axis=2, tiled=True)
        square = jnp.where(kept, band_product(current, right_full), 0.0).astype(jnp.bfloat16)
        cubic = band_product(square, right_full)
        current = jnp.where(kept, 3.0 * square.astype(jnp.float32) - 2.0 * cubic, 0.0).astype(
            jnp.bfloat16
        )
    rows_band = gather_directly(current[:, 1:4], COL, 2)
    near = padded(rows_band, (("row", 0),), 1)
    tiles_here = windows.shape[0]
    points = basis_values.shape[1]
    block_size = near.shape[2]

    def one_tile(tile_index, carry):
        summed, densities = carry
        position = tile_index.astype(jnp.int32)
        start_step = windows[position]
        lead = start_step // 2 - (band_rows * row_index - 1)
        offset = start_step % 2 * step_size
        window_block = window_of(near, lead, offset, functions)
        values = lax.dynamic_index_in_dim(basis_values, position, 0, keepdims=False)
        grads = lax.dynamic_index_in_dim(basis_grads, position, 1, keepdims=False)
        quadrature = lax.dynamic_index_in_dim(weights, position, 0, keepdims=False)
        point_density, contribution = tile_terms(values, grads, quadrature, window_block)
        summed = spread_term(summed, contribution, lead, offset)
        densities = lax.dynamic_update_index_in_dim(densities, point_density, position, 0)
        return (summed, densities)

    start_carry = (
        jnp.zeros((band_rows + 2, 3, block_size, block_size), jnp.float32),
        jnp.zeros((tiles_here, points), jnp.float32),
    )
    local_terms, densities = lax.fori_loop(0, tiles_here, one_tile, start_carry)
    owner_part = scatter_axes(local_terms.astype(jnp.bfloat16), COL, (1, 0), 2).astype(jnp.float32)
    mine = edge_rows(owner_part)
    xc_matrix = jnp.where(kept, jnp.pad(mine, ((0, 0), (1, 1), (0, 0), (0, 0))), 0.0)
    return (current, xc_matrix, densities)


def solution(mesh):
    torus = Mesh(mesh.devices.reshape(mesh.shape["row"], 2, 4), ("row", "col_0", "col_1"))
    placed = (
        P("row", None, COL, None),
        P("row", None),
        P(ROW_COL),
        P(ROW_COL, None, None),
        P(None, ROW_COL, None, None),
        P(ROW_COL, None),
    )
    return jax.shard_map(
        on_device,
        mesh=torus,
        in_specs=placed,
        out_specs=(P("row", None, COL, None), P("row", None, COL, None), P(ROW_COL, None)),
        check_vma=False,
    )
```

profile of v0, /device:TPU:7, one launch (start us, length us, event | category | flops | bytes accessed | tf_op | source)
XLA Modules:
  0.0 434.2 jit_solution(14375397627598703558)
XLA Ops:
  9.1 4.0 collective-permute-start
  15.4 6.5 %collective-permute-done.1 = bf16[2,5,32,256]{3,2,0,1:T(8,128)(2,1)S(1)} collective-permute-done((bf16[2,5,32,256]{3,2,0,1:T(8,128)(2,1)S(1)}, bf16[2,5,32,256]{3,2,0,1:T(8,128)(2,1)S(1)}, u32[]{:S(2)}, u32[]{:S(2)}) %collective-permute-start.1) | collective-permute-done | bytes 163872 | tf_op jit(solution)/shard_map/ppermute | solution.py:31
  22.9 80.5 %all-gather.3.cloned.1.call-done = bf16[8,5,256,256]{3,2,0,1:T(8,128)(2,1)} async-done(((bf16[8,5,32,256]{3,2,0,1:T(8,128)(2,1)}), bf16[8,5,256,256]{3,2,0,1:T(8,128)(2,1)}) %all-gather.3.cloned.1.call-update) | async-done | bytes 5242896 | tf_op jit(solution)/shard_map/all_gather | solution.py:161
  103.4 4.5 %fusion.153 = (bf16[4,5,256,256]{3,2,0,1:T(8,128)(2,1)S(1)}, bf16[4,5,256,256]{3,2,0,1:T(8,128)(2,1)S(1)}, bf16[4,5,256,256]{3,2,0,1:T(8,128)(2,1)S(1)}, bf16[4,5,256,256]{3,2,0,1:T(8,128)(2,1)S(1)}) fusion(bf16[8,5,256,256]{3,2,0,1:T(8,128)(2,1)} %all-gather.3.cloned.1.call-done), kind=kLoop, calls=%fused_computation.165 | loop fusion | bytes 20971520 | tf_op jit(solution)/shard_map/slice | solution.py:106
  114.2 3.6 collective-permute-start.2
  120.0 6.5 %collective-permute-done.3 = bf16[2,5,32,256]{3,2,0,1:T(8,128)(2,1)S(1)} collective-permute-done((bf16[2,5,32,256]{3,2,0,1:T(8,128)(2,1)S(1)}, bf16[2,5,32,256]{3,2,0,1:T(8,128)(2,1)S(1)}, u32[]{:S(2)}, u32[]{:S(2)}) %collective-permute-start.3) | collective-permute-done | bytes 163872 | tf_op jit(solution)/shard_map/ppermute | solution.py:31
  127.5 77.1 %all-gather.5.cloned.1.call-done = bf16[8,5,256,256]{3,2,0,1:T(8,128)(2,1)} async-done(((bf16[8,5,32,256]{3,2,0,1:T(8,128)(2,1)}), bf16[8,5,256,256]{3,2,0,1:T(8,128)(2,1)}) %all-gather.5.cloned.1.call-update) | async-done | bytes 5242896 | tf_op jit(solution)/shard_map/all_gather | solution.py:161
  204.6 4.5 %fusion.152 = (bf16[4,5,256,256]{3,2,0,1:T(8,128)(2,1)S(1)}, bf16[4,5,256,256]{3,2,0,1:T(8,128)(2,1)S(1)}, bf16[4,5,256,256]{3,2,0,1:T(8,128)(2,1)S(1)}, bf16[4,5,256,256]{3,2,0,1:T(8,128)(2,1)S(1)}) fusion(bf16[8,5,256,256]{3,2,0,1:T(8,128)(2,1)} %all-gather.5.cloned.1.call-done), kind=kLoop, calls=%fused_computation.164 | loop fusion | bytes 20971520 | tf_op jit(solution)/shard_map/slice | solution.py:106
  215.6 24.1 %all_to_all.5 = bf16[8,4,3,32,256]{4,3,2,1,0:T(8,128)(2,1)S(1)} all-to-all(bf16[8,4,3,32,256]{4,3,2,1,0:T(8,128)(2,1)S(1)} %broadcast_in_dim.83), channel_id=1, replica_groups=mesh['row'=16,'col_0'=2,'col_1'=4] {'col_0','col_1'}, dimensions={0} | all-to-all | bytes 3145728 | tf_op jit(solution)/shard_map/all_to_all | solution.py:46
  240.0 4.8 %collective-permute-start.4 = (bf16[1,3,256,256]{3,2,1,0:T(8,128)(2,1)S(1)}, bf16[1,3,256,256]{3,2,1,0:T(8,128)(2,1)S(1)}, u32[]{:S(2)}, u32[]{:S(2)}) collective-permute-start(bf16[1,3,256,256]{3,2,1,0:T(8,128)(2,1)S(1)} %bitcast.239), channel_id=1, source_target_pairs={{0,8},{8,16},{16,24},{24,32},{32,40},{40,48},{48,56},{56,64},{64,7... | collective-permute-start | bytes 1179656 | tf_op jit(solution)/shard_map/ppermute | solution.py:29
  249.5 6.5 %collective-permute-done.5 = bf16[1,3,256,256]{3,2,1,0:T(8,128)(2,1)S(1)} collective-permute-done((bf16[1,3,256,256]{3,2,1,0:T(8,128)(2,1)S(1)}, bf16[1,3,256,256]{3,2,1,0:T(8,128)(2,1)S(1)}, u32[]{:S(2)}, u32[]{:S(2)}) %collective-permute-start.5) | collective-permute-done | bytes 393248 | tf_op jit(solution)/shard_map/ppermute | solution.py:31
  260.3 99.6 %while.18 = (s32[]{:T(128)}, f32[6,3,256,256]{3,2,1,0:T(8,128)}, f32[2,4096]{1,0:T(2,128)}, s32[2]{0:T(128)}, s32[]{:T(128)}, /*index=5*/bf16[2,4096,384]{2,1,0:...) while((s32[]{:T(128)}, f32[6,3,256,256]{3,2,1,0:T(8,128)}, ...), condition=%wide.region_5.6_spmd, body=%wide.region_0.5_spmd.sunk | while | flops 2456809472 | bytes 116916952 | solution.py:192
  270.1 7.4 %multiply_reduce_fusion.4 = (f32[4096]{0:T(1024)S(1)}, f32[4096,384]{0,1:T(8,128)}) fusion(bf16[1,4096,384]{1,2,0:T(8,128)(2,1)} %copy.330, s32[]{:T(128)S(6)} %select_n.130, bf16[256,256]{1,0:T(8,128)(2,1)} %get-tuple-element.462, bf16[256,256]{1,0:T(8,128)(2,1)S(1)} %get-tuple-element.463, bf16[256,256]{1,0:T(8,128)(2,1)S(1)} %get-tuple-element.464, ...), kind=kOutput, calls=%fused_computation.6.clone.1 | convolution fusion | flops 1213853696 | bytes 13123588 | tf_op jit(solution)/shard_map/while/body/eval_jaxpr/dot_general | solution.py:84
  277.5 6.6 %copy.331 = f32[4096,384]{1,0:T(8,128)} copy(f32[4096,384]{0,1:T(8,128)} %get-tuple-element.466) | data formatting | bytes 12582912 | tf_op jit(solution)/shard_map/while/body/eval_jaxpr/dot_general | solution.py:84
  284.1 6.8 %fusion.169 = f32[3,4096]{1,0:T(4,128)S(1)} fusion(f32[4096,384]{1,0:T(8,128)} %copy.331, bf16[3,2,4096,384]{3,2,1,0:T(8,128)(2,1)} %get-tuple-element.521, s32[]{:T(128)} %get-tuple-element.495), kind=kLoop, calls=%fused_computation.2.clone.1 | loop fusion | flops 14143488 | bytes 15777796 | tf_op jit(solution)/shard_map/while/body/eval_jaxpr/reduce_sum | solution.py:86
  291.4 9.9 %fusion.170 = f32[4096,384]{1,0:T(8,128)S(1)} fusion(f32[3,4096]{1,0:T(4,128)S(1)} %broadcast_multiply_fusion.5, bf16[3,2,4096,384]{3,2,1,0:T(8,128)(2,1)} %get-tuple-element.521, s32[]{:T(128)} %get-tuple-element.495), kind=kLoop, calls=%fused_computation.3.clone.1 | loop fusion | flops 12582912 | bytes 15777796 | tf_op jit(solution)/shard_map/while/body/eval_jaxpr/reduce_sum | solution.py:91
  319.9 7.3 %multiply_reduce_fusion.4 = (f32[4096]{0:T(1024)S(1)}, f32[4096,384]{0,1:T(8,128)}) fusion(bf16[1,4096,384]{1,2,0:T(8,128)(2,1)} %copy.330, s32[]{:T(128)S(6)} %select_n.130, bf16[256,256]{1,0:T(8,128)(2,1)} %get-tuple-element.462, bf16[256,256]{1,0:T(8,128)(2,1)S(1)} %get-tuple-element.463, bf16[256,256]{1,0:T(8,128)(2,1)S(1)} %get-tuple-element.464, ...), kind=kOutput, calls=%fused_computation.6.clone.1 | convolution fusion | flops 1213853696 | bytes 13123588 | tf_op jit(solution)/shard_map/while/body/eval_jaxpr/dot_general | solution.py:84
  327.2 6.6 %copy.331 = f32[4096,384]{1,0:T(8,128)} copy(f32[4096,384]{0,1:T(8,128)} %get-tuple-element.466) | data formatting | bytes 12582912 | tf_op jit(solution)/shard_map/while/body/eval_jaxpr/dot_general | solution.py:84
  333.8 6.8 %fusion.169 = f32[3,4096]{1,0:T(4,128)S(1)} fusion(f32[4096,384]{1,0:T(8,128)} %copy.331, bf16[3,2,4096,384]{3,2,1,0:T(8,128)(2,1)} %get-tuple-element.521, s32[]{:T(128)} %get-tuple-element.495), kind=kLoop, calls=%fused_computation.2.clone.1 | loop fusion | flops 14143488 | bytes 15777796 | tf_op jit(solution)/shard_map/while/body/eval_jaxpr/reduce_sum | solution.py:86
  341.1 9.9 %fusion.170 = f32[4096,384]{1,0:T(8,128)S(1)} fusion(f32[3,4096]{1,0:T(4,128)S(1)} %broadcast_multiply_fusion.5, bf16[3,2,4096,384]{3,2,1,0:T(8,128)(2,1)} %get-tuple-element.521, s32[]{:T(128)} %get-tuple-element.495), kind=kLoop, calls=%fused_computation.3.clone.1 | loop fusion | flops 12582912 | bytes 15777796 | tf_op jit(solution)/shard_map/while/body/eval_jaxpr/reduce_sum | solution.py:91
  351.1 3.2 fusion.172
  364.3 28.8 %reduce-scatter.3.cloned.1.call-done = bf16[2,6,3,32,256]{4,3,2,1,0:T(8,128)(2,1)} async-done(((bf16[8,6,3,32,256]{4,3,2,1,0:T(8,128)(2,1)}), bf16[2,6,3,32,256]{4,3,2,1,0:T(8,128)(2,1)}) %reduce-scatter.3.cloned.1.call-update) | async-done | bytes 589840 | tf_op jit(solution)/shard_map/reduce_scatter | solution.py:60
  393.2 21.4 %reduce-scatter.5.cloned.1.call-done = bf16[1,6,3,32,256]{4,3,2,1,0:T(8,128)(2,1)} async-done(((bf16[2,6,3,32,256]{4,3,2,1,0:T(8,128)(2,1)}), bf16[1,6,3,32,256]{4,3,2,1,0:T(8,128)(2,1)}) %reduce-scatter.5.cloned.1.call-update) | async-done | bytes 294928 | tf_op jit(solution)/shard_map/reduce_scatter | solution.py:60
  422.1 4.5 %collective-permute-done.7 = bf16[3,32,256]{2,1,0:T(8,128)(2,1)S(1)} collective-permute-done((bf16[3,32,256]{2,1,0:T(8,128)(2,1)S(1)}, bf16[3,32,256]{2,1,0:T(8,128)(2,1)S(1)}, u32[]{:S(2)}, u32[]{:S(2)}) %collective-permute-start.7) | collective-permute-done | bytes 49184 | tf_op jit(solution)/shard_map/ppermute | solution.py:18
  (134 shorter events, 72.7 us)
Async XLA Ops:
  7.2 96.2 %all-gather.3.cloned.1.call-start = ((), (), s32[]{:S(2)}) async-start(), calls=%async_computation.3 | async-start | bytes 5898240 | tf_op jit(solution)/shard_map/all_gather | solution.py:161
  8.0 206.8 %copy-start.9 = (pred[4,5]{0,1:T(8,128)(4,1)}, pred[4,5]{0,1:T(8,128)(4,1)S(1)}, u32[]{:S(2)}) copy-start(pred[4,5]{0,1:T(8,128)(4,1)S(1)} %copy.226) | copy-start | bytes 64
  9.1 6.3 %collective-permute-start = (bf16[2,5,32,256]{3,2,0,1:T(8,128)(2,1)S(1)}, bf16[2,5,32,256]{3,2,0,1:T(8,128)(2,1)S(1)}, u32[]{:S(2)}, u32[]{:S(2)}) collective-permute-start(bf16[2,5,32,256]{3,2,0,1:T(8,128)(2,1)S(1)} %get-tuple-element.389), channel_id=1, source_target_pairs={{0,8},{8,16},{16,24},{24,32},{32,40},{40,48},{48,56},{56,64},{64,7... | collective-permute-start | bytes 491528 | tf_op jit(solution)/shard_map/ppermute | solution.py:29
  13.1 8.7 %collective-permute-start.1 = (bf16[2,5,32,256]{3,2,0,1:T(8,128)(2,1)S(1)}, bf16[2,5,32,256]{3,2,0,1:T(8,128)(2,1)S(1)}, u32[]{:S(2)}, u32[]{:S(2)}) collective-permute-start(bf16[2,5,32,256]{3,2,0,1:T(8,128)(2,1)S(1)} %get-tuple-element.390), channel_id=1, source_target_pairs={{8,0},{16,8},{24,16},{32,24},{40,32},{48,40},{56,48},{64,56},{72,6... | collective-permute-start | bytes 491528 | tf_op jit(solution)/shard_map/ppermute | solution.py:31
  22.8 181.8 %all-gather.5.cloned.1.call-start = ((), (), s32[]{:S(2)}) async-start(), calls=%async_computation.4 | async-start | bytes 5898240 | tf_op jit(solution)/shard_map/all_gather | solution.py:161
  114.2 5.8 %collective-permute-start.2 = (bf16[2,5,32,256]{3,2,0,1:T(8,128)(2,1)S(1)}, bf16[2,5,32,256]{3,2,0,1:T(8,128)(2,1)S(1)}, u32[]{:S(2)}, u32[]{:S(2)}) collective-permute-start(bf16[2,5,32,256]{3,2,0,1:T(8,128)(2,1)S(1)} %get-tuple-element.387), channel_id=1, source_target_pairs={{0,8},{8,16},{16,24},{24,32},{32,40},{40,48},{48,56},{56,64},{64,7... | collective-permute-start | bytes 491528 | tf_op jit(solution)/shard_map/ppermute | solution.py:29
  117.8 8.7 %collective-permute-start.3 = (bf16[2,5,32,256]{3,2,0,1:T(8,128)(2,1)S(1)}, bf16[2,5,32,256]{3,2,0,1:T(8,128)(2,1)S(1)}, u32[]{:S(2)}, u32[]{:S(2)}) collective-permute-start(bf16[2,5,32,256]{3,2,0,1:T(8,128)(2,1)S(1)} %get-tuple-element.388), channel_id=1, source_target_pairs={{8,0},{16,8},{24,16},{32,24},{40,32},{48,40},{56,48},{64,56},{72,6... | collective-permute-start | bytes 491528 | tf_op jit(solution)/shard_map/ppermute | solution.py:31
  127.5 265.7 %reduce-scatter.3.cloned.1.call-start = ((), (), s32[]{:S(2)}) async-start(), calls=%async_computation.5 | async-start | bytes 2949120 | tf_op jit(solution)/shard_map/reduce_scatter | solution.py:60
  215.4 24.4 %copy-start.6 = (bf16[4,5,32,256]{3,2,0,1:T(8,128)(2,1)}, bf16[4,5,32,256]{3,2,0,1:T(8,128)(2,1)S(1)}, u32[]{:S(2)}) copy-start(bf16[4,5,32,256]{3,2,0,1:T(8,128)(2,1)S(1)} %fusion.119) | copy-start | bytes 983044
  239.9 16.1 %copy-start.5 = (bf16[8,4,3,32,256]{4,3,0,2,1:T(8,128)(2,1)}, bf16[8,4,3,32,256]{4,3,0,2,1:T(8,128)(2,1)S(1)}, u32[]{:S(2)}) copy-start(bf16[8,4,3,32,256]{4,3,0,2,1:T(8,128)(2,1)S(1)} %copy.326) | copy-start | bytes 4718596
  240.0 9.5 %collective-permute-start.4 = (bf16[1,3,256,256]{3,2,1,0:T(8,128)(2,1)S(1)}, bf16[1,3,256,256]{3,2,1,0:T(8,128)(2,1)S(1)}, u32[]{:S(2)}, u32[]{:S(2)}) collective-permute-start(bf16[1,3,256,256]{3,2,1,0:T(8,128)(2,1)S(1)} %bitcast.239), channel_id=1, source_target_pairs={{0,8},{8,16},{16,24},{24,32},{32,40},{40,48},{48,56},{56,64},{64,7... | collective-permute-start | bytes 1179656 | tf_op jit(solution)/shard_map/ppermute | solution.py:29
  244.8 11.2 %collective-permute-start.5 = (bf16[1,3,256,256]{3,2,1,0:T(8,128)(2,1)S(1)}, bf16[1,3,256,256]{3,2,1,0:T(8,128)(2,1)S(1)}, u32[]{:S(2)}, u32[]{:S(2)}) collective-permute-start(bf16[1,3,256,256]{3,2,1,0:T(8,128)(2,1)S(1)} %bitcast.238), channel_id=1, source_target_pairs={{8,0},{16,8},{24,16},{32,24},{40,32},{48,40},{56,48},{64,56},{72,6... | collective-permute-start | bytes 1179656 | tf_op jit(solution)/shard_map/ppermute | solution.py:31
  260.3 4.6 %copy-start.3 = (bf16[6,3,256,256]{3,2,1,0:T(8,128)(2,1)}, bf16[6,3,256,256]{3,2,1,0:T(8,128)(2,1)S(1)}, u32[]{:S(2)}) copy-start(bf16[6,3,256,256]{3,2,1,0:T(8,128)(2,1)S(1)} %get-tuple-element.520) | copy-start | bytes 7077892 | tf_op jit(solution)/shard_map/while
  284.1 6.9 %copy-start.8 = (f32[2,4096]{1,0:T(2,128)S(1)}, f32[2,4096]{1,0:T(2,128)}, u32[]{:S(2)}) copy-start(f32[2,4096]{1,0:T(2,128)} %get-tuple-element.522) | copy-start | bytes 98308 | tf_op jit(solution)/shard_map/while
  306.4 3.7 copy-start.4
  310.1 4.6 %copy-start.3 = (bf16[6,3,256,256]{3,2,1,0:T(8,128)(2,1)}, bf16[6,3,256,256]{3,2,1,0:T(8,128)(2,1)S(1)}, u32[]{:S(2)}) copy-start(bf16[6,3,256,256]{3,2,1,0:T(8,128)(2,1)S(1)} %get-tuple-element.520) | copy-start | bytes 7077892 | tf_op jit(solution)/shard_map/while
  333.8 6.9 %copy-start.8 = (f32[2,4096]{1,0:T(2,128)S(1)}, f32[2,4096]{1,0:T(2,128)}, u32[]{:S(2)}) copy-start(f32[2,4096]{1,0:T(2,128)} %get-tuple-element.522) | copy-start | bytes 98308 | tf_op jit(solution)/shard_map/while
  356.1 3.0 copy-start.11
  356.1 3.7 copy-start.4
  364.2 54.1 %copy-start.7 = (bf16[4,5,32,256]{3,2,0,1:T(8,128)(2,1)S(1)}, bf16[4,5,32,256]{3,2,0,1:T(8,128)(2,1)}, u32[]{:S(2)}) copy-start(bf16[4,5,32,256]{3,2,0,1:T(8,128)(2,1)} %copy-done.6) | copy-start | bytes 983044
  364.3 62.4 %copy-start.10 = (pred[4,5]{0,1:T(8,128)(4,1)S(1)}, pred[4,5]{0,1:T(8,128)(4,1)}, u32[]{:S(2)}) copy-start(pred[4,5]{0,1:T(8,128)(4,1)} %copy-done.9) | copy-start | bytes 64
  364.3 50.3 %reduce-scatter.5.cloned.1.call-start = ((), (), s32[]{:S(2)}) async-start(), calls=%async_computation.6 | async-start | bytes 884736 | tf_op jit(solution)/shard_map/reduce_scatter | solution.py:60
  415.4 6.7 %collective-permute-start.6 = (bf16[3,32,256]{2,1,0:T(8,128)(2,1)S(1)}, bf16[3,32,256]{2,1,0:T(8,128)(2,1)S(1)}, u32[]{:S(2)}, u32[]{:S(2)}) collective-permute-start(bf16[3,32,256]{2,1,0:T(8,128)(2,1)S(1)} %get-tuple-element.391), channel_id=1, source_target_pairs={{0,8},{8,16},{16,24},{24,32},{32,40},{40,48},{48,56},{56,64},{64,7... | collective-permute-start | bytes 147464 | tf_op jit(solution)/shard_map/ppermute | solution.py:18
  419.1 7.5 %collective-permute-start.7 = (bf16[3,32,256]{2,1,0:T(8,128)(2,1)S(1)}, bf16[3,32,256]{2,1,0:T(8,128)(2,1)S(1)}, u32[]{:S(2)}, u32[]{:S(2)}) collective-permute-start(bf16[3,32,256]{2,1,0:T(8,128)(2,1)S(1)} %get-tuple-element.392), channel_id=1, source_target_pairs={{8,0},{16,8},{24,16},{32,24},{40,32},{48,40},{56,48},{64,56},{72,6... | collective-permute-start | bytes 147464 | tf_op jit(solution)/shard_map/ppermute | solution.py:18
  (7 other events, 12.1 us)
Sparse Core Ops, SparseCore 0:
  22.9 80.3 all-gather.2
  127.6 76.9 all-gather.4
  364.4 28.7 reduce-scatter.2
  395.4 19.1 reduce-scatter.4
where the time goes:
time: 435 us; the launch traced here: 434 us
  waiting for transfers between devices  235 us (54%)
  local copies, waits for them, and re-layouts  52 us (12%)
  other arithmetic  49.7 us (11%)
  matrix products  30.2 us (7%)
  blocking collectives  24.1 us (6%)
  starting transfers between devices  23.4 us (5%)
  between operations  14.1 us (3%)
  loops' own time  5.52 us (1%)
    all_gather x2, waiting for transfers between devices, on_device(): right_full = lax.all_gather(near_right, COL, axis=2, tiled=True)  158 us
    reduce_scatter x2, waiting for transfers between devices, sum_in_order(): pieces = lax.psum_scatter(pieces, axes[k], scatter_dimension=0, tiled=True)  50.2 us
    all_to_all x1, blocking collectives, sent_to_all(): lax.all_to_all(jnp.broadcast_to(value[None], (length, *value.shape)), axi...  24.1 us
    reduce_sum x2, other arithmetic, tile_terms(): jnp.sum(((2.0 * by_gradient * scaled)[None] * slopes)[:, :, None] * grads...  19.9 us
    ppermute x3, waiting for transfers between devices, padded(): lax.ppermute(head, axis, [((i + 1) % count, i) for i in range(ends)])  19.5 us
    dot_general x2, matrix products, tile_terms(): jnp.dot(values, window_block, preferred_element_type=jnp.float32)  14.7 us
    reduce_sum x2, other arithmetic, tile_terms(): jnp.sum(projected[None] * grads.astype(jnp.float32), axis=2)  13.6 us
    dot_general x2, local copies, waits for them, and re-layouts, tile_terms(): jnp.dot(values, window_block, preferred_element_type=jnp.float32)  13.1 us
  transfers between devices with their start and end apart: 12, of which 11 were waited for; matrix products, arithmetic and copies ran while one was open for 0% of the time, Pallas kernels for 0%

commit v1 on v0

--- a/solution.py
+++ b/solution.py
@@ -3,6 +3,7 @@
 from jax import lax
 from jax.sharding import Mesh
 from jax.sharding import PartitionSpec as P
+from jax.lax import all_to_all, axis_size
 
 ITERS = 2
 COL = ("col_0", "col_1")
@@ -158,7 +159,15 @@
     current = jnp.where(kept, density, jnp.zeros_like(density))
     for iteration in range(ITERS):
         near_right = padded(current, (("row", 0),), 2)
-        right_full = lax.all_gather(near_right, COL, axis=2, tiled=True)
+        right_full = jnp.concatenate(
+            all_to_all(
+                jnp.stack([near_right for _ in range(axis_size(COL))], 0),
+                axis_name=COL,
+                split_axis=0,
+                concat_axis=0,
+            ),
+            2,
+        )
         square = jnp.where(kept, band_product(current, right_full), 0.0).astype(jnp.bfloat16)
         cubic = band_product(square, right_full)
         current = jnp.where(kept, 3.0 * square.astype(jnp.float32) - 2.0 * cubic, 0.0).astype(

time: 435 us -> 401 us (0.922)
  waiting for transfers between devices: 235 us -> 79.1 us
  blocking collectives: 24.1 us -> 148 us
    all_gather x2 -> x0, waiting for transfers between devices: 158 us -> none  [on_device(): right_full = lax.all_gather(near_right, COL, axis=2, tiled=True)]
    all_to_all x0 -> x2, blocking collectives: none -> 127 us  [on_device(): all_to_all(jnp.stack([near_right for _ in range(axis_size(COL))], 0), axi...]
    slice x2 -> x12, local copies, waits for them, and re-layouts: 9.04 us -> 7.41 us  [band_product(): shifted = right_padded[offset_step:offset_step + blocks]]
  transfers between devices with their start and end apart: 12 -> 10, of which waited for: 11 -> 9; matrix products, arithmetic and copies ran while one was open for 0% -> 0% of each run, Pallas kernels for 0% -> 0%
where the time goes in v1:
time: 401 us; the launch traced here: 400 us
  blocking collectives  148 us (37%)
  waiting for transfers between devices  79.1 us (20%)
  local copies, waits for them, and re-layouts  49.2 us (12%)
  other arithmetic  48.1 us (12%)
  matrix products  30.3 us (8%)
  starting transfers between devices  26.2 us (7%)
  between operations  14.5 us (4%)
  loops' own time  5.51 us (1%)
    all_to_all x2, blocking collectives, on_device(): all_to_all(jnp.stack([near_right for _ in range(axis_size(COL))], 0), axi...  127 us
    reduce_scatter x2, waiting for transfers between devices, sum_in_order(): pieces = lax.psum_scatter(pieces, axes[k], scatter_dimension=0, tiled=True)  50.5 us
    all_to_all x1, blocking collectives, sent_to_all(): lax.all_to_all(jnp.broadcast_to(value[None], (length, *value.shape)), axi...  20.9 us
    ppermute x3, waiting for transfers between devices, padded(): lax.ppermute(head, axis, [((i + 1) % count, i) for i in range(ends)])  20.8 us
    reduce_sum x2, other arithmetic, tile_terms(): jnp.sum(((2.0 * by_gradient * scaled)[None] * slopes)[:, :, None] * grads...  19.9 us
    ppermute x3, starting transfers between devices, padded(): lax.ppermute(tail, axis, [(i, (i + 1) % count) for i in range(ends)])  15.2 us
    dot_general x2, matrix products, tile_terms(): jnp.dot(values, window_block, preferred_element_type=jnp.float32)  14.7 us
    reduce_sum x2, other arithmetic, tile_terms(): jnp.sum(projected[None] * grads.astype(jnp.float32), axis=2)  13.6 us
  transfers between devices with their start and end apart: 10, of which 9 were waited for; matrix products, arithmetic and copies ran while one was open for 0% of the time, Pallas kernels for 0%

profile of v1, /device:TPU:7, one launch (start us, length us, event | category | flops | bytes accessed | tf_op | source)
XLA Modules:
  0.0 400.3 jit_solution(4066017568430894158)
XLA Ops:
  9.1 4.0 %collective-permute-start = (bf16[2,5,32,256]{3,2,0,1:T(8,128)(2,1)S(1)}, bf16[2,5,32,256]{3,2,0,1:T(8,128)(2,1)S(1)}, u32[]{:S(2)}, u32[]{:S(2)}) collective-permute-start(bf16[2,5,32,256]{3,2,0,1:T(8,128)(2,1)S(1)} %get-tuple-element.391), channel_id=1, source_target_pairs={{0,8},{8,16},{16,24},{24,32},{32,40},{40,48},{48,56},{56,64},{64,7... | collective-permute-start | bytes 491528 | tf_op jit(solution)/shard_map/ppermute | solution.py:30
  15.4 6.5 %collective-permute-done.1 = bf16[2,5,32,256]{3,2,0,1:T(8,128)(2,1)S(1)} collective-permute-done((bf16[2,5,32,256]{3,2,0,1:T(8,128)(2,1)S(1)}, bf16[2,5,32,256]{3,2,0,1:T(8,128)(2,1)S(1)}, u32[]{:S(2)}, u32[]{:S(2)}) %collective-permute-start.1) | collective-permute-done | bytes 163872 | tf_op jit(solution)/shard_map/ppermute | solution.py:32
  22.7 67.1 %all_to_all.15 = bf16[8,8,5,32,256]{4,3,2,1,0:T(8,128)(2,1)S(1)} all-to-all(bf16[8,8,5,32,256]{4,3,2,1,0:T(8,128)(2,1)S(1)} %stack.121), channel_id=1, replica_groups=mesh['row'=16,'col_0'=2,'col_1'=4] {'col_0','col_1'}, dimensions={0} | all-to-all | bytes 10485760 | tf_op jit(solution)/shard_map/all_to_all | solution.py:163
  98.2 3.3 collective-permute-start.2
  103.8 7.8 %collective-permute-done.3 = bf16[2,5,32,256]{3,2,0,1:T(8,128)(2,1)S(1)} collective-permute-done((bf16[2,5,32,256]{3,2,0,1:T(8,128)(2,1)S(1)}, bf16[2,5,32,256]{3,2,0,1:T(8,128)(2,1)S(1)}, u32[]{:S(2)}, u32[]{:S(2)}) %collective-permute-start.3) | collective-permute-done | bytes 163872 | tf_op jit(solution)/shard_map/ppermute | solution.py:32
  112.4 59.6 %all_to_all.16 = bf16[8,8,5,32,256]{4,3,2,1,0:T(8,128)(2,1)S(1)} all-to-all(bf16[8,8,5,32,256]{4,3,2,1,0:T(8,128)(2,1)S(1)} %stack.122), channel_id=1, replica_groups=mesh['row'=16,'col_0'=2,'col_1'=4] {'col_0','col_1'}, dimensions={0} | all-to-all | bytes 10485760 | tf_op jit(solution)/shard_map/all_to_all | solution.py:163
  181.3 20.9 %all_to_all.17 = bf16[8,4,3,32,256]{4,3,2,1,0:T(8,128)(2,1)S(1)} all-to-all(bf16[8,4,3,32,256]{4,3,2,1,0:T(8,128)(2,1)S(1)} %broadcast_in_dim.83), channel_id=1, replica_groups=mesh['row'=16,'col_0'=2,'col_1'=4] {'col_0','col_1'}, dimensions={0} | all-to-all | bytes 3145728 | tf_op jit(solution)/shard_map/all_to_all | solution.py:47
  202.4 7.9 %collective-permute-start.4 = (bf16[1,3,256,256]{3,2,1,0:T(8,128)(2,1)S(1)}, bf16[1,3,256,256]{3,2,1,0:T(8,128)(2,1)S(1)}, u32[]{:S(2)}, u32[]{:S(2)}) collective-permute-start(bf16[1,3,256,256]{3,2,1,0:T(8,128)(2,1)S(1)} %bitcast.273), channel_id=1, source_target_pairs={{0,8},{8,16},{16,24},{24,32},{32,40},{40,48},{48,56},{56,64},{64,7... | collective-permute-start | bytes 1179656 | tf_op jit(solution)/shard_map/ppermute | solution.py:30
  215.0 6.5 %collective-permute-done.5 = bf16[1,3,256,256]{3,2,1,0:T(8,128)(2,1)S(1)} collective-permute-done((bf16[1,3,256,256]{3,2,1,0:T(8,128)(2,1)S(1)}, bf16[1,3,256,256]{3,2,1,0:T(8,128)(2,1)S(1)}, u32[]{:S(2)}, u32[]{:S(2)}) %collective-permute-start.5) | collective-permute-done | bytes 393248 | tf_op jit(solution)/shard_map/ppermute | solution.py:32
  225.8 99.6 %while.18 = (s32[]{:T(128)}, f32[6,3,256,256]{3,2,1,0:T(8,128)}, f32[2,4096]{1,0:T(2,128)}, s32[2]{0:T(128)}, s32[]{:T(128)}, /*index=5*/bf16[2,4096,384]{2,1,0:...) while((s32[]{:T(128)}, f32[6,3,256,256]{3,2,1,0:T(8,128)}, ...), condition=%wide.region_5.6_spmd, body=%wide.region_0.5_spmd.sunk | while | flops 2456809472 | bytes 116916952 | solution.py:201
  232.6 3.0 copy.354
  235.7 7.4 %multiply_reduce_fusion.4 = (f32[4096]{0:T(1024)S(1)}, f32[4096,384]{0,1:T(8,128)}) fusion(bf16[1,4096,384]{1,2,0:T(8,128)(2,1)} %copy.354, s32[]{:T(128)S(6)} %select_n.130, bf16[256,256]{1,0:T(8,128)(2,1)} %get-tuple-element.464, bf16[256,256]{1,0:T(8,128)(2,1)S(1)} %get-tuple-element.465, bf16[256,256]{1,0:T(8,128)(2,1)S(1)} %get-tuple-element.466, ...), kind=kOutput, calls=%fused_computation.6.clone.1 | convolution fusion | flops 1213853696 | bytes 13123588 | tf_op jit(solution)/shard_map/while/body/eval_jaxpr/dot_general | solution.py:85
  243.0 6.6 %copy.355 = f32[4096,384]{1,0:T(8,128)} copy(f32[4096,384]{0,1:T(8,128)} %get-tuple-element.468) | data formatting | bytes 12582912 | tf_op jit(solution)/shard_map/while/body/eval_jaxpr/dot_general | solution.py:85
  249.6 6.8 %fusion.177 = f32[3,4096]{1,0:T(4,128)S(1)} fusion(f32[4096,384]{1,0:T(8,128)} %copy.355, bf16[3,2,4096,384]{3,2,1,0:T(8,128)(2,1)} %get-tuple-element.523, s32[]{:T(128)} %get-tuple-element.497), kind=kLoop, calls=%fused_computation.2.clone.1 | loop fusion | flops 14143488 | bytes 15777796 | tf_op jit(solution)/shard_map/while/body/eval_jaxpr/reduce_sum | solution.py:87
  256.9 9.9 %fusion.178 = f32[4096,384]{1,0:T(8,128)S(1)} fusion(f32[3,4096]{1,0:T(4,128)S(1)} %broadcast_multiply_fusion.5, bf16[3,2,4096,384]{3,2,1,0:T(8,128)(2,1)} %get-tuple-element.523, s32[]{:T(128)} %get-tuple-element.497), kind=kLoop, calls=%fused_computation.3.clone.1 | loop fusion | flops 12582912 | bytes 15777796 | tf_op jit(solution)/shard_map/while/body/eval_jaxpr/reduce_sum | solution.py:92
  266.9 3.2 fusion.180
  285.5 7.3 %multiply_reduce_fusion.4 = (f32[4096]{0:T(1024)S(1)}, f32[4096,384]{0,1:T(8,128)}) fusion(bf16[1,4096,384]{1,2,0:T(8,128)(2,1)} %copy.354, s32[]{:T(128)S(6)} %select_n.130, bf16[256,256]{1,0:T(8,128)(2,1)} %get-tuple-element.464, bf16[256,256]{1,0:T(8,128)(2,1)S(1)} %get-tuple-element.465, bf16[256,256]{1,0:T(8,128)(2,1)S(1)} %get-tuple-element.466, ...), kind=kOutput, calls=%fused_computation.6.clone.1 | convolution fusion | flops 1213853696 | bytes 13123588 | tf_op jit(solution)/shard_map/while/body/eval_jaxpr/dot_general | solution.py:85
  292.8 6.6 %copy.355 = f32[4096,384]{1,0:T(8,128)} copy(f32[4096,384]{0,1:T(8,128)} %get-tuple-element.468) | data formatting | bytes 12582912 | tf_op jit(solution)/shard_map/while/body/eval_jaxpr/dot_general | solution.py:85
  299.4 6.8 %fusion.177 = f32[3,4096]{1,0:T(4,128)S(1)} fusion(f32[4096,384]{1,0:T(8,128)} %copy.355, bf16[3,2,4096,384]{3,2,1,0:T(8,128)(2,1)} %get-tuple-element.523, s32[]{:T(128)} %get-tuple-element.497), kind=kLoop, calls=%fused_computation.2.clone.1 | loop fusion | flops 14143488 | bytes 15777796 | tf_op jit(solution)/shard_map/while/body/eval_jaxpr/reduce_sum | solution.py:87
  306.7 9.9 %fusion.178 = f32[4096,384]{1,0:T(8,128)S(1)} fusion(f32[3,4096]{1,0:T(4,128)S(1)} %broadcast_multiply_fusion.5, bf16[3,2,4096,384]{3,2,1,0:T(8,128)(2,1)} %get-tuple-element.523, s32[]{:T(128)} %get-tuple-element.497), kind=kLoop, calls=%fused_computation.3.clone.1 | loop fusion | flops 12582912 | bytes 15777796 | tf_op jit(solution)/shard_map/while/body/eval_jaxpr/reduce_sum | solution.py:92
  316.7 3.2 fusion.180
  329.9 29.0 %reduce-scatter.3.cloned.1.call-done = bf16[2,6,3,32,256]{4,3,2,1,0:T(8,128)(2,1)} async-done(((bf16[8,6,3,32,256]{4,3,2,1,0:T(8,128)(2,1)}), bf16[2,6,3,32,256]{4,3,2,1,0:T(8,128)(2,1)}) %reduce-scatter.3.cloned.1.call-update) | async-done | bytes 589840 | tf_op jit(solution)/shard_map/reduce_scatter | solution.py:61
  358.9 21.5 %reduce-scatter.5.cloned.1.call-done = bf16[1,6,3,32,256]{4,3,2,1,0:T(8,128)(2,1)} async-done(((bf16[2,6,3,32,256]{4,3,2,1,0:T(8,128)(2,1)}), bf16[1,6,3,32,256]{4,3,2,1,0:T(8,128)(2,1)}) %reduce-scatter.5.cloned.1.call-update) | async-done | bytes 294928 | tf_op jit(solution)/shard_map/reduce_scatter | solution.py:61
  388.0 4.5 %collective-permute-done.7 = bf16[3,32,256]{2,1,0:T(8,128)(2,1)S(1)} collective-permute-done((bf16[3,32,256]{2,1,0:T(8,128)(2,1)S(1)}, bf16[3,32,256]{2,1,0:T(8,128)(2,1)S(1)}, u32[]{:S(2)}, u32[]{:S(2)}) %collective-permute-start.7) | collective-permute-done | bytes 49184 | tf_op jit(solution)/shard_map/ppermute | solution.py:19
  (140 shorter events, 70.9 us)
Async XLA Ops:
  7.2 351.7 %reduce-scatter.3.cloned.1.call-start = ((), (), s32[]{:S(2)}) async-start(), calls=%async_computation.5 | async-start | bytes 2949120 | tf_op jit(solution)/shard_map/reduce_scatter | solution.py:61
  8.0 171.9 %copy-start.7 = (pred[4,5]{0,1:T(8,128)(4,1)}, pred[4,5]{0,1:T(8,128)(4,1)S(1)}, u32[]{:S(2)}) copy-start(pred[4,5]{0,1:T(8,128)(4,1)S(1)} %copy.164) | copy-start | bytes 64
  9.1 6.3 %collective-permute-start = (bf16[2,5,32,256]{3,2,0,1:T(8,128)(2,1)S(1)}, bf16[2,5,32,256]{3,2,0,1:T(8,128)(2,1)S(1)}, u32[]{:S(2)}, u32[]{:S(2)}) collective-permute-start(bf16[2,5,32,256]{3,2,0,1:T(8,128)(2,1)S(1)} %get-tuple-element.391), channel_id=1, source_target_pairs={{0,8},{8,16},{16,24},{24,32},{32,40},{40,48},{48,56},{56,64},{64,7... | collective-permute-start | bytes 491528 | tf_op jit(solution)/shard_map/ppermute | solution.py:30
  13.1 8.7 %collective-permute-start.1 = (bf16[2,5,32,256]{3,2,0,1:T(8,128)(2,1)S(1)}, bf16[2,5,32,256]{3,2,0,1:T(8,128)(2,1)S(1)}, u32[]{:S(2)}, u32[]{:S(2)}) collective-permute-start(bf16[2,5,32,256]{3,2,0,1:T(8,128)(2,1)S(1)} %get-tuple-element.392), channel_id=1, source_target_pairs={{8,0},{16,8},{24,16},{32,24},{40,32},{48,40},{56,48},{64,56},{72,6... | collective-permute-start | bytes 491528 | tf_op jit(solution)/shard_map/ppermute | solution.py:32
  98.2 5.6 %collective-permute-start.2 = (bf16[2,5,32,256]{3,2,0,1:T(8,128)(2,1)S(1)}, bf16[2,5,32,256]{3,2,0,1:T(8,128)(2,1)S(1)}, u32[]{:S(2)}, u32[]{:S(2)}) collective-permute-start(bf16[2,5,32,256]{3,2,0,1:T(8,128)(2,1)S(1)} %get-tuple-element.389), channel_id=1, source_target_pairs={{0,8},{8,16},{16,24},{24,32},{32,40},{40,48},{48,56},{56,64},{64,7... | collective-permute-start | bytes 491528 | tf_op jit(solution)/shard_map/ppermute | solution.py:30
  101.6 10.0 %collective-permute-start.3 = (bf16[2,5,32,256]{3,2,0,1:T(8,128)(2,1)S(1)}, bf16[2,5,32,256]{3,2,0,1:T(8,128)(2,1)S(1)}, u32[]{:S(2)}, u32[]{:S(2)}) collective-permute-start(bf16[2,5,32,256]{3,2,0,1:T(8,128)(2,1)S(1)} %get-tuple-element.390), channel_id=1, source_target_pairs={{8,0},{16,8},{24,16},{32,24},{40,32},{48,40},{56,48},{64,56},{72,6... | collective-permute-start | bytes 491528 | tf_op jit(solution)/shard_map/ppermute | solution.py:32
  202.3 19.2 %copy-start.3 = (bf16[8,4,3,32,256]{4,3,0,2,1:T(8,128)(2,1)}, bf16[8,4,3,32,256]{4,3,0,2,1:T(8,128)(2,1)S(1)}, u32[]{:S(2)}) copy-start(bf16[8,4,3,32,256]{4,3,0,2,1:T(8,128)(2,1)S(1)} %copy.350) | copy-start | bytes 4718596
  202.4 12.6 %collective-permute-start.4 = (bf16[1,3,256,256]{3,2,1,0:T(8,128)(2,1)S(1)}, bf16[1,3,256,256]{3,2,1,0:T(8,128)(2,1)S(1)}, u32[]{:S(2)}, u32[]{:S(2)}) collective-permute-start(bf16[1,3,256,256]{3,2,1,0:T(8,128)(2,1)S(1)} %bitcast.273), channel_id=1, source_target_pairs={{0,8},{8,16},{16,24},{24,32},{32,40},{40,48},{48,56},{56,64},{64,7... | collective-permute-start | bytes 1179656 | tf_op jit(solution)/shard_map/ppermute | solution.py:30
  210.3 11.2 %collective-permute-start.5 = (bf16[1,3,256,256]{3,2,1,0:T(8,128)(2,1)S(1)}, bf16[1,3,256,256]{3,2,1,0:T(8,128)(2,1)S(1)}, u32[]{:S(2)}, u32[]{:S(2)}) collective-permute-start(bf16[1,3,256,256]{3,2,1,0:T(8,128)(2,1)S(1)} %bitcast.272), channel_id=1, source_target_pairs={{8,0},{16,8},{24,16},{32,24},{40,32},{48,40},{56,48},{64,56},{72,6... | collective-permute-start | bytes 1179656 | tf_op jit(solution)/shard_map/ppermute | solution.py:32
  225.8 4.6 %copy-start.1 = (bf16[6,3,256,256]{3,2,1,0:T(8,128)(2,1)}, bf16[6,3,256,256]{3,2,1,0:T(8,128)(2,1)S(1)}, u32[]{:S(2)}) copy-start(bf16[6,3,256,256]{3,2,1,0:T(8,128)(2,1)S(1)} %get-tuple-element.522) | copy-start | bytes 7077892 | tf_op jit(solution)/shard_map/while
  249.6 6.9 %copy-start.6 = (f32[2,4096]{1,0:T(2,128)S(1)}, f32[2,4096]{1,0:T(2,128)}, u32[]{:S(2)}) copy-start(f32[2,4096]{1,0:T(2,128)} %get-tuple-element.524) | copy-start | bytes 98308 | tf_op jit(solution)/shard_map/while
  270.1 1.5 copy-start
  271.9 3.0 copy-start.9
  272.0 3.7 copy-start.2
  275.7 4.6 %copy-start.1 = (bf16[6,3,256,256]{3,2,1,0:T(8,128)(2,1)}, bf16[6,3,256,256]{3,2,1,0:T(8,128)(2,1)S(1)}, u32[]{:S(2)}) copy-start(bf16[6,3,256,256]{3,2,1,0:T(8,128)(2,1)S(1)} %get-tuple-element.522) | copy-start | bytes 7077892 | tf_op jit(solution)/shard_map/while
  299.4 6.9 %copy-start.6 = (f32[2,4096]{1,0:T(2,128)S(1)}, f32[2,4096]{1,0:T(2,128)}, u32[]{:S(2)}) copy-start(f32[2,4096]{1,0:T(2,128)} %get-tuple-element.524) | copy-start | bytes 98308 | tf_op jit(solution)/shard_map/while
  319.9 1.5 copy-start
  321.7 2.9 copy-start.9
  321.7 3.7 copy-start.2
  329.8 54.4 %copy-start.5 = (bf16[4,5,32,256]{3,2,0,1:T(8,128)(2,1)S(1)}, bf16[4,5,32,256]{3,2,0,1:T(8,128)(2,1)}, u32[]{:S(2)}) copy-start(bf16[4,5,32,256]{3,2,0,1:T(8,128)(2,1)} %copy-done.4) | copy-start | bytes 983044
  329.8 62.7 %copy-start.8 = (pred[4,5]{0,1:T(8,128)(4,1)S(1)}, pred[4,5]{0,1:T(8,128)(4,1)}, u32[]{:S(2)}) copy-start(pred[4,5]{0,1:T(8,128)(4,1)} %copy-done.7) | copy-start | bytes 64
  329.8 50.6 %reduce-scatter.5.cloned.1.call-start = ((), (), s32[]{:S(2)}) async-start(), calls=%async_computation.6 | async-start | bytes 884736 | tf_op jit(solution)/shard_map/reduce_scatter | solution.py:61
  381.2 6.7 %collective-permute-start.6 = (bf16[3,32,256]{2,1,0:T(8,128)(2,1)S(1)}, bf16[3,32,256]{2,1,0:T(8,128)(2,1)S(1)}, u32[]{:S(2)}, u32[]{:S(2)}) collective-permute-start(bf16[3,32,256]{2,1,0:T(8,128)(2,1)S(1)} %get-tuple-element.393), channel_id=1, source_target_pairs={{0,8},{8,16},{16,24},{24,32},{32,40},{40,48},{48,56},{56,64},{64,7... | collective-permute-start | bytes 147464 | tf_op jit(solution)/shard_map/ppermute | solution.py:19
  385.0 7.5 %collective-permute-start.7 = (bf16[3,32,256]{2,1,0:T(8,128)(2,1)S(1)}, bf16[3,32,256]{2,1,0:T(8,128)(2,1)S(1)}, u32[]{:S(2)}, u32[]{:S(2)}) collective-permute-start(bf16[3,32,256]{2,1,0:T(8,128)(2,1)S(1)} %get-tuple-element.394), channel_id=1, source_target_pairs={{8,0},{16,8},{24,16},{32,24},{40,32},{48,40},{56,48},{64,56},{72,6... | collective-permute-start | bytes 147464 | tf_op jit(solution)/shard_map/ppermute | solution.py:19
  (3 other events, 2.0 us)
Sparse Core Ops, SparseCore 0:
  330.0 28.8 reduce-scatter.2
  361.2 19.1 reduce-scatter.4
